TPU v7x, 32 devices: a whole 2x2x4 slice. The times are simulated.
32 devices in a mesh: gx: 4 (over x, core), gy: 2 (over y), gz: 4 (over z).
Axes of the slice: x: 2, y: 2, z: 4, core: 2. Of those that a mesh axis runs over, the one named last changes fastest.
Arguments:
- offsets: float32 [3, 4, 4, 8, 128], P(None, 'gx', 'gy', 'gz'), may hold values from 0 to 11, as said below
- type_ids: int32 [4, 4, 8, 128], P('gx', 'gy', 'gz'), may hold values from 0 to 1
- neighbours: int32 [4, 4, 8, 27], P('gx', 'gy', 'gz'), may hold values from 0 to 48, as said below
- type_chi: float32 [2], replicated, may hold values from 3 to 7
- type_eta: float32 [2], replicated, may hold values from 6 to 12
- type_gamma: float32 [2], replicated, may hold values from 0.5 to 1
Outputs:
- charges: float32 [4, 4, 8, 128], P('gx', 'gy', 'gz')
- residuals: float32 [2, 4, 4, 8, 128], P(None, 'gx', 'gy', 'gz')
Inputs may be any that keep to these rules, and one draw needn't show every extreme that they name: `neighbours`: each tile's row lists the tile itself and some of the 26 cells around it, each at most once, as indices into its device's block padded by one cell on every side (3) x (4) x (4) in first-dimension-major order; unused slots hold (3) * 4 * 4. Two tiles list each other with opposite displacements or not at all. `offsets`: any two atoms of the box lie at least 0.8 A apart.
All inputs are finite; a program needn't handle non-finite values.
Results may differ from a plain program's by a relative error of at most 0.0003.
Values sent between devices are 32-bit elements; how exact they have to be, the bound alone decides.
A program may use at most 64 MiB of HBM per device.

v0:
```python
import jax
import jax.numpy as jnp
from jax import lax
from jax.sharding import PartitionSpec as P

ITERS = 3


CELL_EDGE = 11.0
CUTOFF = 10.0
COULOMB = 14.4


def extended(cells, sides, width):
    for axis, dim in sides:
        count = lax.axis_size(axis)
        head = lax.slice_in_dim(cells, 0, width, axis=dim)
        tail = lax.slice_in_dim(cells, cells.shape[dim] - width, cells.shape[dim], axis=dim)
        cells = jnp.concatenate(
            [
                lax.ppermute(tail, axis, [(i, (i + 1) % count) for i in range(count)]),
                cells,
                lax.ppermute(head, axis, [((i + 1) % count, i) for i in range(count)]),
            ],
            axis=dim,
        )
    return cells


def taper_value(distance):
    scaled = distance / CUTOFF
    squared = scaled * scaled
    return 1.0 + squared * squared * (-35.0 + scaled * (84.0 + scaled * (-70.0 + scaled * 20.0)))


def couplings(own_pos, own_shield, near_pos, near_shield, shifts, listed, itself):
    displace = near_pos[:, :, None, :] + shifts[:, :, None, None] - own_pos[:, None, :, None]
    dist_sq = jnp.sum(displace * displace, axis=0)
    distance = jnp.sqrt(dist_sq)
    screen = own_shield[None, :, None] * near_shield[:, None, :]
    kernel = COULOMB * taper_value(distance) / jnp.cbrt(dist_sq * distance + screen)
    diagonal_mask = jnp.eye(own_pos.shape[1], dtype=bool)
    retained = (
        listed[:, None, None]
        & (distance < CUTOFF)
        & jnp.logical_not(itself[:, None, None] & diagonal_mask[None])
    )
    return jnp.where(retained, kernel, jnp.zeros_like(kernel))


def table_lookup(type_ids, table):
    result = jnp.zeros(type_ids.shape, table.dtype)
    for kind_index in range(table.shape[0]):
        result = jnp.where(type_ids == kind_index, table[kind_index], result)
    return result


def decode_cells(entries, local_one, local_two, local_three, width_two, width_three):
    plane_cells = (width_two + 2) * (width_three + 2)
    step_one = entries // plane_cells - 1 - local_one[..., None]
    step_two = entries // (width_three + 2) % (width_two + 2) - 1 - local_two[..., None]
    step_three = entries % (width_three + 2) - 1 - local_three[..., None]
    return (step_one, step_two, step_three)


def summed_over(values):
    return jnp.sum(values, axis=(1, 2))


def per_device(offsets, type_ids, neighbours, type_chi, type_eta, type_gamma):
    cells_one, cells_two, cells_three, atoms_tile = offsets.shape[1:]
    tiles = cells_one * cells_two * cells_three
    slots = neighbours.shape[-1]
    sentinel = (cells_one + 2) * (cells_two + 2) * (cells_three + 2)
    chi_atom = table_lookup(type_ids, type_chi)
    eta_atom = table_lookup(type_ids, type_eta)
    shield = table_lookup(type_ids, type_gamma ** (-1.5))
    source = jnp.stack([-chi_atom, -jnp.ones_like(chi_atom)])
    fields = jnp.concatenate([offsets, shield[None]], 0)
    padded = extended(fields, (("gx", 1), ("gy", 2), ("gz", 3)), 1)
    source_ghosts = extended(source, (("gx", 1), ("gy", 2), ("gz", 3)), 1)

    def flatten(stacked):
        reshaped = stacked.reshape(stacked.shape[0], sentinel, atoms_tile)
        return jnp.concatenate(
            [reshaped, jnp.zeros((stacked.shape[0], 1, atoms_tile), stacked.dtype)], 1
        )

    pos_all = flatten(padded[0:3])
    shield_all = flatten(padded[3:4])[0]
    shape_grid = (cells_one, cells_two, cells_three)
    local_one = jnp.broadcast_to(jnp.arange(cells_one, dtype=jnp.int32)[:, None, None], shape_grid)
    local_two = jnp.broadcast_to(jnp.arange(cells_two, dtype=jnp.int32)[None, :, None], shape_grid)
    local_three = jnp.broadcast_to(
        jnp.arange(cells_three, dtype=jnp.int32)[None, None, :], shape_grid
    )
    step_one, step_two, step_three = decode_cells(
        neighbours, local_one, local_two, local_three, cells_two, cells_three
    )
    listed = (neighbours != sentinel).reshape(tiles, slots)
    itself = ((step_one == 0) & (step_two == 0) & (step_three == 0)).reshape(tiles, slots)
    shifts = (
        jnp.stack([step_one, step_two, step_three], axis=-2)
        .reshape(tiles, 3, slots)
        .astype(jnp.float32)
        * CELL_EDGE
    )
    row_index = neighbours.reshape(tiles, slots)
    own_pos = jnp.moveaxis(offsets.reshape(3, tiles, atoms_tile), 1, 0)
    own_shield = shield.reshape(tiles, atoms_tile)

    def build_tile(tile_item):
        own_block, own_screen, indices, shifted, valid_slot, selfish = tile_item
        return couplings(
            own_block,
            own_screen,
            pos_all[:, indices],
            shield_all[indices],
            shifted,
            valid_slot,
            selfish,
        )

    blocks = lax.map(build_tile, (own_pos, own_shield, row_index, shifts, listed, itself))
    diagonal = eta_atom.reshape(tiles, atoms_tile)

    def apply_padded(local_part, ghosts):
        values = flatten(ghosts)[:, row_index]
        return diagonal[None] * local_part + jnp.einsum(
            "tsij,ctsj->cti", blocks, values, precision=lax.Precision.HIGHEST
        )

    def products(residual, image_now, solution, direction):
        return lax.psum(
            (
                summed_over(residual * residual),
                summed_over(residual * image_now),
                summed_over(solution),
                summed_over(residual),
                summed_over(direction),
            ),
            ("gx", "gy", "gz"),
        )

    residual = source.reshape(2, tiles, atoms_tile)
    solution = jnp.zeros_like(residual)
    image_now = apply_padded(residual, source_ghosts)
    norm_now, curvature, unused_one, unused_two, unused_three = products(
        residual, image_now, solution, residual
    )
    step_size = norm_now / curvature
    direction = residual
    along_image = image_now
    carried = (norm_now, norm_now, norm_now, norm_now, step_size)
    for iteration in range(ITERS):
        solution = solution + step_size[:, None, None] * direction
        residual = residual - step_size[:, None, None] * along_image
        if iteration + 1 < ITERS:
            shaped = residual.reshape(2, cells_one, cells_two, cells_three, atoms_tile)
            apply_ghosts = extended(shaped, (("gx", 1), ("gy", 2), ("gz", 3)), 1)
            image_now = apply_padded(residual, apply_ghosts)
            norm_next, curvature, sum_solution, sum_residual, sum_direction = products(
                residual, image_now, solution, direction
            )
            growth = norm_next / norm_now
            step_size = norm_next / (curvature - growth * norm_next / step_size)
            direction = residual + growth[:, None, None] * direction
            along_image = image_now + growth[:, None, None] * along_image
            norm_now = norm_next
            carried = (sum_solution, sum_residual, sum_direction, growth, step_size)
    sum_solution, sum_residual, sum_direction, growth, last_step = carried
    totals = sum_solution + last_step * (sum_residual + growth * sum_direction)
    charges = 1000.0 * (solution[0] - totals[0] / totals[1] * solution[1])
    return (
        charges.reshape(cells_one, cells_two, cells_three, atoms_tile),
        residual.reshape(2, cells_one, cells_two, cells_three, atoms_tile),
    )


def solution(mesh):
    placed = (
        P(None, "gx", "gy", "gz", None),
        P("gx", "gy", "gz", None),
        P("gx", "gy", "gz", None),
        P(),
        P(),
        P(),
    )
    return jax.shard_map(
        per_device,
        mesh=mesh,
        in_specs=placed,
        out_specs=(P("gx", "gy", "gz", None), P(None, "gx", "gy", "gz", None)),
        check_vma=False,
    )
```

profile of v0, /device:TPU:0, one launch (start us, length us, event | category | flops | bytes accessed | tf_op | source)
XLA Modules:
  0.0 240.6 jit_solution(7625335458110972850)
XLA Ops:
  1.9 1.4 fusion.55
  3.3 1.3 fusion.54
  4.6 4.4 %select_select_fusion = (f32[1,2,2,128]{3,2,1,0:T(2,128)S(1)}, f32[1,2,2,128]{3,2,1,0:T(2,128)S(1)}, f32[1,1,2,2,128]{4,3,2,1,0:T(2,128)S(1)}) fusion(f32[]{:T(128)} %bitcast.22, f32[]{:T(128)} %bitcast.21, s32[1,2,2,128]{3,2,1,0:T(2,128)} %param.9, f32[]{:T(128)} %bitcast.14, f32[]{:T(128)} %bitcast.13, f32[]{:T(128)} %bitcast.10, f32[]{:T(128)} %bitcast.9), kind=kLoop, calls=%fused_computation.102 | loop fusion | flops 4608 | bytes 8216 | tf_op jit(solution)/shard_map/jit(_where)/select_n | solution.py:54
  9.0 0.7 pad_maximum_fusion.12
  10.2 2.0 collective-permute-start.7
  12.9 1.1 collective-permute-start.1
  14.0 0.7 compare_and_fusion
  15.5 0.7 copy.26
  16.3 2.4 collective-permute-start.2
  18.7 0.7 pad_maximum_fusion.6
  19.5 2.0 collective-permute-start.8
  21.6 0.7 collective-permute-done.3
  22.3 1.6 collective-permute-start.4
  23.9 2.2 collective-permute-start.5
  26.2 0.7 pad_maximum_fusion.2
  27.6 3.3 %collective-permute-start.11 = (f32[4,3,4,1,128]{4,3,2,1,0:T(1,128)S(1)}, f32[4,3,4,1,128]{4,3,2,1,0:T(1,128)S(1)}, u32[]{:S(2)}, u32[]{:S(2)}) collective-permute-start(f32[4,3,4,1,128]{4,3,2,1,0:T(1,128)S(1)} %get-tuple-element.215), channel_id=1, source_target_pairs={{1,0},{2,1},{3,2},{0,3},{5,4},{6,5},{7,6},{4,7},{9,8},{10,9},{11,1... | collective-permute-start | bytes 73736 | tf_op jit(solution)/shard_map/ppermute | solution.py:23
  31.0 0.7 gather_fusion.2
  31.7 1.0 collective-permute-done.10
  32.7 0.8 pad_maximum_fusion
  33.5 29.4 %while.12 = (s32[]{:T(128)}, f32[4,27,128,128]{3,2,1,0:T(8,128)}, pred[4,27]{1,0:T(4,128)(4,1)S(1)}, s32[4,27]{1,0:T(4,128)}, f32[3,49,128]{2,0,1:T(4,128)S(1)},...) while((s32[]{:T(128)}, f32[4,27,128,128]{3,2,1,0:T(8,128)}, ...), condition=%wide.region_4.5_spmd, body=%wide.region_2.4_spmd.sunk | while | flops 13298899 | bytes 5686811 | solution.py:124
  36.4 4.5 %fusion.67 = f32[4,27,128,128]{3,2,1,0:T(8,128)} fusion(f32[4,27,128,128]{3,2,1,0:T(8,128)} %get-tuple-element.328, s32[]{:T(128)} %get-tuple-element.327, f32[27,128,128]{2,1,0:T(8,128)S(1)} %multiply_reduce_fusion.7, f32[27,128]{1,0:T(8,128)S(1)} %gather_fusion.1, f32[128]{0:T(128)S(1)} %fusion.66, pred[27]{0:T(512)(128)(4,1)S(1)} %get-tuple-element.314, ...), kind=kLoop, calls=%fused_computation.21.clone.1 | loop fusion | flops 9732096 | bytes 3570230 | tf_op jit(solution)/shard_map/while/body/jit(dynamic_update_index_in_dim)/dynamic_update_slice | solution.py:124
  43.8 4.5 %fusion.67 = f32[4,27,128,128]{3,2,1,0:T(8,128)} fusion(f32[4,27,128,128]{3,2,1,0:T(8,128)} %get-tuple-element.328, s32[]{:T(128)} %get-tuple-element.327, f32[27,128,128]{2,1,0:T(8,128)S(1)} %multiply_reduce_fusion.7, f32[27,128]{1,0:T(8,128)S(1)} %gather_fusion.1, f32[128]{0:T(128)S(1)} %fusion.66, pred[27]{0:T(512)(128)(4,1)S(1)} %get-tuple-element.314, ...), kind=kLoop, calls=%fused_computation.21.clone.1 | loop fusion | flops 9732096 | bytes 3570230 | tf_op jit(solution)/shard_map/while/body/jit(dynamic_update_index_in_dim)/dynamic_update_slice | solution.py:124
  51.1 4.5 %fusion.67 = f32[4,27,128,128]{3,2,1,0:T(8,128)} fusion(f32[4,27,128,128]{3,2,1,0:T(8,128)} %get-tuple-element.328, s32[]{:T(128)} %get-tuple-element.327, f32[27,128,128]{2,1,0:T(8,128)S(1)} %multiply_reduce_fusion.7, f32[27,128]{1,0:T(8,128)S(1)} %gather_fusion.1, f32[128]{0:T(128)S(1)} %fusion.66, pred[27]{0:T(512)(128)(4,1)S(1)} %get-tuple-element.314, ...), kind=kLoop, calls=%fused_computation.21.clone.1 | loop fusion | flops 9732096 | bytes 3570230 | tf_op jit(solution)/shard_map/while/body/jit(dynamic_update_index_in_dim)/dynamic_update_slice | solution.py:124
  58.4 4.5 %fusion.67 = f32[4,27,128,128]{3,2,1,0:T(8,128)} fusion(f32[4,27,128,128]{3,2,1,0:T(8,128)} %get-tuple-element.328, s32[]{:T(128)} %get-tuple-element.327, f32[27,128,128]{2,1,0:T(8,128)S(1)} %multiply_reduce_fusion.7, f32[27,128]{1,0:T(8,128)S(1)} %gather_fusion.1, f32[128]{0:T(128)S(1)} %fusion.66, pred[27]{0:T(512)(128)(4,1)S(1)} %get-tuple-element.314, ...), kind=kLoop, calls=%fused_computation.21.clone.1 | loop fusion | flops 9732096 | bytes 3570230 | tf_op jit(solution)/shard_map/while/body/jit(dynamic_update_index_in_dim)/dynamic_update_slice | solution.py:124
  62.9 8.3 %fusion.24 = (f32[2]{0:T(128)S(1)}, f32[2,4,128]{2,0,1:T(2,128)S(1)}) fusion(f32[2,1,2,2,128]{4,0,3,2,1:T(2,128)S(1)} %copy.23, f32[2,4,128]{2,0,1:T(2,128)S(1)} %bitcast_multiply_fusion.3, f32[2,4,27,128]{3,0,2,1:T(2,128)S(1)} %bitcast.129, f32[4,27,128,128]{3,2,1,0:T(8,128)} %get-tuple-element.127), kind=kOutput, calls=%fused_computation.72 | convolution fusion | flops 42470400 | bytes 7200776 | tf_op jit(solution)/shard_map/tsij,ctsj->cti/dot_general | solution.py:129
  71.2 39.8 %all-reduce.8 = (f32[2]{0:T(128)S(1)}, f32[2]{0:T(128)S(1)}) all-reduce(f32[2]{0:T(128)S(1)} %get-tuple-element.233, f32[2]{0:T(128)S(1)} %get-tuple-element.247), channel_id=1, replica_groups=mesh['gx'=4,'gy'=2,'gz'=4] {'gx','gy','gz'}, use_global_device_ids=true, to_apply=%region_1.2 | all-reduce | flops 4 | bytes 32 | tf_op jit(solution)/shard_map/psum | solution.py:134
  111.1 1.7 collective-permute-start.13
  112.9 1.3 collective-permute-done.12
  114.2 2.3 collective-permute-start.14
  116.6 1.5 collective-permute-done.14
  118.1 2.0 collective-permute-done.15
  120.2 2.2 collective-permute-start.16
  122.4 1.7 collective-permute-start.17
  124.1 1.7 collective-permute-done.16
  126.1 0.7 gather_fusion.3
  126.9 8.3 %multiply_reduce_fusion.3 = (f32[2]{0:T(128)S(1)}, f32[2]{0:T(128)S(1)}, f32[2,4,128]{2,0,1:T(2,128)S(1)}) fusion(f32[2,4,128]{2,0,1:T(2,128)S(1)} %bitcast_subtract_fusion, f32[2,4,27,128]{3,0,2,1:T(2,128)S(1)} %bitcast.131, f32[4,27,128,128]{3,2,1,0:T(8,128)} %get-tuple-element.127, f32[4,128]{1,0:T(4,128)S(1)} %bitcast.155), kind=kOutput, calls=%fused_computation.81 | convolution fusion | flops 42473468 | bytes 7198736 | tf_op jit(solution)/shard_map/tsij,ctsj->cti/dot_general | solution.py:129
  135.2 39.1 %all-reduce.7 = (f32[2]{0:T(128)S(1)}, f32[2]{0:T(128)S(1)}) all-reduce(f32[2]{0:T(128)S(1)} %get-tuple-element.168, f32[2]{0:T(128)S(1)} %get-tuple-element.167), channel_id=1, replica_groups=mesh['gx'=4,'gy'=2,'gz'=4] {'gx','gy','gz'}, use_global_device_ids=true, to_apply=%region_8.9 | all-reduce | flops 4 | bytes 32 | tf_op jit(solution)/shard_map/psum | solution.py:134
  174.5 1.7 collective-permute-start.19
  176.3 1.3 collective-permute-done.18
  177.6 2.3 collective-permute-start.20
  180.0 1.5 collective-permute-done.20
  181.5 2.0 collective-permute-done.21
  183.6 1.9 collective-permute-start.22
  185.5 1.9 collective-permute-start.23
  187.7 1.5 collective-permute-done.22
  189.3 0.7 gather_fusion.4
  190.1 8.3 %fusion.35 = (f32[2]{0:T(128)S(1)}, f32[2]{0:T(128)S(1)}, f32[2]{0:T(128)S(1)}, f32[2,4,128]{2,0,1:T(2,128)S(1)}) fusion(f32[2,4,128]{2,0,1:T(2,128)S(1)} %get-tuple-element.232, f32[2,4,27,128]{3,0,2,1:T(2,128)S(1)} %bitcast.130, f32[4,27,128,128]{3,2,1,0:T(8,128)} %get-tuple-element.127, f32[4,128]{1,0:T(4,128)S(1)} %bitcast.156), kind=kOutput, calls=%fused_computation.116 | convolution fusion | flops 42474488 | bytes 7198744 | tf_op jit(solution)/shard_map/tsij,ctsj->cti/dot_general | solution.py:129
  198.4 39.0 %all-reduce.6 = (f32[2]{0:T(128)S(1)}, f32[2]{0:T(128)S(1)}, f32[2]{0:T(128)S(1)}, f32[2]{0:T(128)S(1)}, f32[2]{0:T(128)S(1)}) all-reduce(f32[2]{0:T(128)S(1)} %get-tuple-element.166, f32[2]{0:T(128)S(1)} %get-tuple-element.165, f32[2]{0:T(128)S(1)} %get-tuple-element.203, ...), channel_id=1, replica_groups=mesh['gx'=4,'gy'=2,'gz'=4] {'gx','gy','gz'}, use_global_device_ids=true, to_apply=%region_12.13 | all-reduce | flops 10 | bytes 80 | tf_op jit(solution)/shard_map/psum | solution.py:134
  (127 shorter events, 18.8 us)
Async XLA Ops:
  9.7 9.0 %collective-permute-start.6 = (f32[4,1,2,2,128]{4,3,2,1,0:T(2,128)S(1)}, f32[4,1,2,2,128]{4,3,2,1,0:T(2,128)S(1)}, u32[]{:S(2)}, u32[]{:S(2)}) collective-permute-start(f32[4,1,2,2,128]{4,3,2,1,0:T(2,128)S(1)} %pad_maximum_fusion.12), channel_id=1, source_target_pairs={{0,8},{8,16},{16,24},{24,0},{1,9},{9,17},{17,25},{25,1},{2,10},{10... | collective-permute-start | bytes 24584 | tf_op jit(solution)/shard_map/ppermute | solution.py:21
  10.2 8.5 %collective-permute-start.7 = (f32[4,1,2,2,128]{4,3,2,1,0:T(2,128)S(1)}, f32[4,1,2,2,128]{4,3,2,1,0:T(2,128)S(1)}, u32[]{:S(2)}, u32[]{:S(2)}) collective-permute-start(f32[4,1,2,2,128]{4,3,2,1,0:T(2,128)S(1)} %pad_maximum_fusion.12), channel_id=1, source_target_pairs={{8,0},{16,8},{24,16},{0,24},{9,1},{17,9},{25,17},{1,25},{10,2},{18... | collective-permute-start | bytes 24584 | tf_op jit(solution)/shard_map/ppermute | solution.py:23
  12.2 4.0 %collective-permute-start = (f32[2,1,2,2,128]{4,3,2,1,0:T(2,128)S(1)}, f32[2,1,2,2,128]{4,3,2,1,0:T(2,128)S(1)}, u32[]{:S(2)}, u32[]{:S(2)}) collective-permute-start(f32[2,1,2,2,128]{4,3,2,1,0:T(2,128)S(1)} %get-tuple-element.234), channel_id=1, source_target_pairs={{0,8},{8,16},{16,24},{24,0},{1,9},{9,17},{17,25},{25,1},{2,10},{10... | collective-permute-start | bytes 12296 | tf_op jit(solution)/shard_map/ppermute | solution.py:21
  12.9 3.4 %collective-permute-start.1 = (f32[2,1,2,2,128]{4,3,2,1,0:T(2,128)S(1)}, f32[2,1,2,2,128]{4,3,2,1,0:T(2,128)S(1)}, u32[]{:S(2)}, u32[]{:S(2)}) collective-permute-start(f32[2,1,2,2,128]{4,3,2,1,0:T(2,128)S(1)} %get-tuple-element.234), channel_id=1, source_target_pairs={{8,0},{16,8},{24,16},{0,24},{9,1},{17,9},{25,17},{1,25},{10,2},{18... | collective-permute-start | bytes 12296 | tf_op jit(solution)/shard_map/ppermute | solution.py:23
  16.3 5.3 %collective-permute-start.2 = (f32[2,3,1,2,128]{4,3,2,1,0:T(2,128)S(1)}, f32[2,3,1,2,128]{4,3,2,1,0:T(2,128)S(1)}, u32[]{:S(2)}, u32[]{:S(2)}) collective-permute-start(f32[2,3,1,2,128]{4,3,2,1,0:T(2,128)S(1)} %get-tuple-element.228), channel_id=1, source_target_pairs={{0,4},{4,0},{1,5},{5,1},{2,6},{6,2},{3,7},{7,3},{8,12},{12,8},{9,1... | collective-permute-start | bytes 18440 | tf_op jit(solution)/shard_map/ppermute | solution.py:21
  18.6 3.6 %collective-permute-start.3 = (f32[2,3,1,2,128]{4,3,2,1,0:T(2,128)S(1)}, f32[2,3,1,2,128]{4,3,2,1,0:T(2,128)S(1)}, u32[]{:S(2)}, u32[]{:S(2)}) collective-permute-start(f32[2,3,1,2,128]{4,3,2,1,0:T(2,128)S(1)} %get-tuple-element.229), channel_id=1, source_target_pairs={{4,0},{0,4},{5,1},{1,5},{6,2},{2,6},{7,3},{3,7},{12,8},{8,12},{13,... | collective-permute-start | bytes 18440 | tf_op jit(solution)/shard_map/ppermute | solution.py:23
  19.5 6.7 %collective-permute-start.8 = (f32[4,3,1,2,128]{4,3,2,1,0:T(2,128)S(1)}, f32[4,3,1,2,128]{4,3,2,1,0:T(2,128)S(1)}, u32[]{:S(2)}, u32[]{:S(2)}) collective-permute-start(f32[4,3,1,2,128]{4,3,2,1,0:T(2,128)S(1)} %get-tuple-element.220), channel_id=1, source_target_pairs={{0,4},{4,0},{1,5},{5,1},{2,6},{6,2},{3,7},{7,3},{8,12},{12,8},{9,1... | collective-permute-start | bytes 36872 | tf_op jit(solution)/shard_map/ppermute | solution.py:21
  21.5 4.7 %collective-permute-start.9 = (f32[4,3,1,2,128]{4,3,2,1,0:T(2,128)S(1)}, f32[4,3,1,2,128]{4,3,2,1,0:T(2,128)S(1)}, u32[]{:S(2)}, u32[]{:S(2)}) collective-permute-start(f32[4,3,1,2,128]{4,3,2,1,0:T(2,128)S(1)} %get-tuple-element.221), channel_id=1, source_target_pairs={{4,0},{0,4},{5,1},{1,5},{6,2},{2,6},{7,3},{3,7},{12,8},{8,12},{13,... | collective-permute-start | bytes 36872 | tf_op jit(solution)/shard_map/ppermute | solution.py:23
  22.3 8.5 %collective-permute-start.4 = (f32[2,3,4,1,128]{4,3,2,1,0:T(1,128)S(1)}, f32[2,3,4,1,128]{4,3,2,1,0:T(1,128)S(1)}, u32[]{:S(2)}, u32[]{:S(2)}) collective-permute-start(f32[2,3,4,1,128]{4,3,2,1,0:T(1,128)S(1)} %get-tuple-element.222), channel_id=1, source_target_pairs={{0,1},{1,2},{2,3},{3,0},{4,5},{5,6},{6,7},{7,4},{8,9},{9,10},{10,1... | collective-permute-start | bytes 36872 | tf_op jit(solution)/shard_map/ppermute | solution.py:21
  23.9 6.9 %collective-permute-start.5 = (f32[2,3,4,1,128]{4,3,2,1,0:T(1,128)S(1)}, f32[2,3,4,1,128]{4,3,2,1,0:T(1,128)S(1)}, u32[]{:S(2)}, u32[]{:S(2)}) collective-permute-start(f32[2,3,4,1,128]{4,3,2,1,0:T(1,128)S(1)} %get-tuple-element.223), channel_id=1, source_target_pairs={{1,0},{2,1},{3,2},{0,3},{5,4},{6,5},{7,6},{4,7},{9,8},{10,9},{11,1... | collective-permute-start | bytes 36872 | tf_op jit(solution)/shard_map/ppermute | solution.py:23
  27.0 5.7 %collective-permute-start.10 = (f32[4,3,4,1,128]{4,3,2,1,0:T(1,128)S(1)}, f32[4,3,4,1,128]{4,3,2,1,0:T(1,128)S(1)}, u32[]{:S(2)}, u32[]{:S(2)}) collective-permute-start(f32[4,3,4,1,128]{4,3,2,1,0:T(1,128)S(1)} %get-tuple-element.214), channel_id=1, source_target_pairs={{0,1},{1,2},{2,3},{3,0},{4,5},{5,6},{6,7},{7,4},{8,9},{9,10},{10,1... | collective-permute-start | bytes 73736 | tf_op jit(solution)/shard_map/ppermute | solution.py:21
  27.6 5.1 %collective-permute-start.11 = (f32[4,3,4,1,128]{4,3,2,1,0:T(1,128)S(1)}, f32[4,3,4,1,128]{4,3,2,1,0:T(1,128)S(1)}, u32[]{:S(2)}, u32[]{:S(2)}) collective-permute-start(f32[4,3,4,1,128]{4,3,2,1,0:T(1,128)S(1)} %get-tuple-element.215), channel_id=1, source_target_pairs={{1,0},{2,1},{3,2},{0,3},{5,4},{6,5},{7,6},{4,7},{9,8},{10,9},{11,1... | collective-permute-start | bytes 73736 | tf_op jit(solution)/shard_map/ppermute | solution.py:23
  111.1 3.0 %collective-permute-start.12 = (f32[2,1,2,2,128]{4,0,3,2,1:T(2,128)S(1)}, f32[2,1,2,2,128]{4,0,3,2,1:T(2,128)S(1)}, u32[]{:S(2)}, u32[]{:S(2)}) collective-permute-start(f32[2,1,2,2,128]{4,0,3,2,1:T(2,128)S(1)} %bitcast.142), channel_id=1, source_target_pairs={{0,8},{8,16},{16,24},{24,0},{1,9},{9,17},{17,25},{25,1},{2,10},{10... | collective-permute-start | bytes 12296 | tf_op jit(solution)/shard_map/ppermute | solution.py:21
  111.1 3.1 %collective-permute-start.13 = (f32[2,1,2,2,128]{4,0,3,2,1:T(2,128)S(1)}, f32[2,1,2,2,128]{4,0,3,2,1:T(2,128)S(1)}, u32[]{:S(2)}, u32[]{:S(2)}) collective-permute-start(f32[2,1,2,2,128]{4,0,3,2,1:T(2,128)S(1)} %bitcast.143), channel_id=1, source_target_pairs={{8,0},{16,8},{24,16},{0,24},{9,1},{17,9},{25,17},{1,25},{10,2},{18... | collective-permute-start | bytes 12296 | tf_op jit(solution)/shard_map/ppermute | solution.py:23
  114.2 3.9 %collective-permute-start.14 = (f32[2,3,1,2,128]{4,0,3,2,1:T(2,128)S(1)}, f32[2,3,1,2,128]{4,0,3,2,1:T(2,128)S(1)}, u32[]{:S(2)}, u32[]{:S(2)}) collective-permute-start(f32[2,3,1,2,128]{4,0,3,2,1:T(2,128)S(1)} %get-tuple-element.226), channel_id=1, source_target_pairs={{0,4},{4,0},{1,5},{5,1},{2,6},{6,2},{3,7},{7,3},{8,12},{12,8},{9,1... | collective-permute-start | bytes 18440 | tf_op jit(solution)/shard_map/ppermute | solution.py:21
  116.5 3.6 %collective-permute-start.15 = (f32[2,3,1,2,128]{4,0,3,2,1:T(2,128)S(1)}, f32[2,3,1,2,128]{4,0,3,2,1:T(2,128)S(1)}, u32[]{:S(2)}, u32[]{:S(2)}) collective-permute-start(f32[2,3,1,2,128]{4,0,3,2,1:T(2,128)S(1)} %get-tuple-element.227), channel_id=1, source_target_pairs={{4,0},{0,4},{5,1},{1,5},{6,2},{2,6},{7,3},{3,7},{12,8},{8,12},{13,... | collective-permute-start | bytes 18440 | tf_op jit(solution)/shard_map/ppermute | solution.py:23
  120.2 5.5 %collective-permute-start.16 = (f32[2,3,4,1,128]{4,0,3,2,1:T(2,128)S(1)}, f32[2,3,4,1,128]{4,0,3,2,1:T(2,128)S(1)}, u32[]{:S(2)}, u32[]{:S(2)}) collective-permute-start(f32[2,3,4,1,128]{4,0,3,2,1:T(2,128)S(1)} %get-tuple-element.218), channel_id=1, source_target_pairs={{0,1},{1,2},{2,3},{3,0},{4,5},{5,6},{6,7},{7,4},{8,9},{9,10},{10,1... | collective-permute-start | bytes 36872 | tf_op jit(solution)/shard_map/ppermute | solution.py:21
  122.4 3.7 %collective-permute-start.17 = (f32[2,3,4,1,128]{4,0,3,2,1:T(2,128)S(1)}, f32[2,3,4,1,128]{4,0,3,2,1:T(2,128)S(1)}, u32[]{:S(2)}, u32[]{:S(2)}) collective-permute-start(f32[2,3,4,1,128]{4,0,3,2,1:T(2,128)S(1)} %get-tuple-element.219), channel_id=1, source_target_pairs={{1,0},{2,1},{3,2},{0,3},{5,4},{6,5},{7,6},{4,7},{9,8},{10,9},{11,1... | collective-permute-start | bytes 36872 | tf_op jit(solution)/shard_map/ppermute | solution.py:23
  174.5 3.1 %collective-permute-start.18 = (f32[2,1,2,2,128]{4,0,3,2,1:T(2,128)S(1)}, f32[2,1,2,2,128]{4,0,3,2,1:T(2,128)S(1)}, u32[]{:S(2)}, u32[]{:S(2)}) collective-permute-start(f32[2,1,2,2,128]{4,0,3,2,1:T(2,128)S(1)} %bitcast.137), channel_id=1, source_target_pairs={{0,8},{8,16},{16,24},{24,0},{1,9},{9,17},{17,25},{25,1},{2,10},{10... | collective-permute-start | bytes 12296 | tf_op jit(solution)/shard_map/ppermute | solution.py:21
  174.5 3.1 %collective-permute-start.19 = (f32[2,1,2,2,128]{4,0,3,2,1:T(2,128)S(1)}, f32[2,1,2,2,128]{4,0,3,2,1:T(2,128)S(1)}, u32[]{:S(2)}, u32[]{:S(2)}) collective-permute-start(f32[2,1,2,2,128]{4,0,3,2,1:T(2,128)S(1)} %bitcast.138), channel_id=1, source_target_pairs={{8,0},{16,8},{24,16},{0,24},{9,1},{17,9},{25,17},{1,25},{10,2},{18... | collective-permute-start | bytes 12296 | tf_op jit(solution)/shard_map/ppermute | solution.py:23
  177.6 3.9 %collective-permute-start.20 = (f32[2,3,1,2,128]{4,0,3,2,1:T(2,128)S(1)}, f32[2,3,1,2,128]{4,0,3,2,1:T(2,128)S(1)}, u32[]{:S(2)}, u32[]{:S(2)}) collective-permute-start(f32[2,3,1,2,128]{4,0,3,2,1:T(2,128)S(1)} %get-tuple-element.224), channel_id=1, source_target_pairs={{0,4},{4,0},{1,5},{5,1},{2,6},{6,2},{3,7},{7,3},{8,12},{12,8},{9,1... | collective-permute-start | bytes 18440 | tf_op jit(solution)/shard_map/ppermute | solution.py:21
  179.9 3.6 %collective-permute-start.21 = (f32[2,3,1,2,128]{4,0,3,2,1:T(2,128)S(1)}, f32[2,3,1,2,128]{4,0,3,2,1:T(2,128)S(1)}, u32[]{:S(2)}, u32[]{:S(2)}) collective-permute-start(f32[2,3,1,2,128]{4,0,3,2,1:T(2,128)S(1)} %get-tuple-element.225), channel_id=1, source_target_pairs={{4,0},{0,4},{5,1},{1,5},{6,2},{2,6},{7,3},{3,7},{12,8},{8,12},{13,... | collective-permute-start | bytes 18440 | tf_op jit(solution)/shard_map/ppermute | solution.py:23
  183.6 5.5 %collective-permute-start.22 = (f32[2,3,4,1,128]{4,0,3,2,1:T(2,128)S(1)}, f32[2,3,4,1,128]{4,0,3,2,1:T(2,128)S(1)}, u32[]{:S(2)}, u32[]{:S(2)}) collective-permute-start(f32[2,3,4,1,128]{4,0,3,2,1:T(2,128)S(1)} %get-tuple-element.216), channel_id=1, source_target_pairs={{0,1},{1,2},{2,3},{3,0},{4,5},{5,6},{6,7},{7,4},{8,9},{9,10},{10,1... | collective-permute-start | bytes 36872 | tf_op jit(solution)/shard_map/ppermute | solution.py:21
  185.5 3.7 %collective-permute-start.23 = (f32[2,3,4,1,128]{4,0,3,2,1:T(2,128)S(1)}, f32[2,3,4,1,128]{4,0,3,2,1:T(2,128)S(1)}, u32[]{:S(2)}, u32[]{:S(2)}) collective-permute-start(f32[2,3,4,1,128]{4,0,3,2,1:T(2,128)S(1)} %get-tuple-element.217), channel_id=1, source_target_pairs={{1,0},{2,1},{3,2},{0,3},{5,4},{6,5},{7,6},{4,7},{9,8},{10,9},{11,1... | collective-permute-start | bytes 36872 | tf_op jit(solution)/shard_map/ppermute | solution.py:23
where the time goes:
time: 242 us; the launch traced here: 241 us
  blocking collectives  118 us (49%)
  other arithmetic  33.9 us (14%)
  starting transfers between devices  32.6 us (13%)
  matrix products  25 us (10%)
  waiting for transfers between devices  15.1 us (6%)
  local copies, waits for them, and re-layouts  13.6 us (6%)
    psum x3, blocking collectives, products(): lax.psum((summed_over(residual * residual), summed_over(residual * image_...  118 us
    dot_general x3, matrix products, apply_padded(): jnp.einsum('tsij,ctsj->cti', blocks, values, precision=lax.Precision.HIGH...  25 us
    dynamic_update_slice x4, other arithmetic, per_device(): lax.map(build_tile, (own_pos, own_shield, row_index, shifts, listed, itse...  17.9 us
    ppermute x12, starting transfers between devices, extended(): lax.ppermute(tail, axis, [(i, (i + 1) % count) for i in range(count)])  16.5 us
    ppermute x12, starting transfers between devices, extended(): lax.ppermute(head, axis, [((i + 1) % count, i) for i in range(count)])  16.1 us
    ppermute x12, waiting for transfers between devices, extended(): lax.ppermute(tail, axis, [(i, (i + 1) % count) for i in range(count)])  9.78 us
    ppermute x12, waiting for transfers between devices, extended(): lax.ppermute(head, axis, [((i + 1) % count, i) for i in range(count)])  5.32 us
  transfers between devices with their start and end apart: 24, of which 12 were waited for; matrix products, arithmetic and copies ran while one was open for 2% of the time, Pallas kernels for 0%

commit v1 on v0

v1 whole, which is shorter than its diff:
```python
import itertools

import jax
import jax.numpy as jnp
from jax import lax
from jax.experimental import pallas as pl
from jax.experimental.pallas import tpu as pltpu
from jax.sharding import PartitionSpec as P

ITERS = 3
CELL_EDGE = 11.0
CUTOFF = 10.0
COULOMB = 14.4
AXES = ("gx", "gy", "gz")
FAR = 1000.0
MESH = pl.DeviceIdType.MESH
STEPS = [d for d in itertools.product((-1, 0, 1), repeat=3)]
REMOTE = [d for d in STEPS if d != (0, 0, 0)]


def rounded_sides(step, cells):
    source, target = [], []
    for d, c in zip(step, cells):
        if d == 0:
            source.append(pl.ds(1, c))
            target.append(pl.ds(1, c))
        elif d > 0:
            source.append(pl.ds(c, 1))
            target.append(pl.ds(0, 1))
        else:
            source.append(pl.ds(1, 1))
            target.append(pl.ds(c + 1, 1))
    return tuple(source), tuple(target)


def make_kernel(sizes, groups, cells, atoms, types, rows):
    width = tuple(c + 2 for c in cells)
    tiles = cells[0] * cells[1] * cells[2]
    local = list(itertools.product(*[range(c) for c in cells]))
    padded = list(itertools.product(*[range(w) for w in width]))
    own = tuple(slice(1, 1 + c) for c in cells)
    group_sizes = []
    for axes in groups:
        count = 1
        for a in axes:
            count = count * sizes[a]
        group_sizes.append(count)

    def linear(place):
        return (place[0] * width[1] + place[1]) * width[2] + place[2]

    def kernel(*refs):
        off_ref, type_ref, list_ref, chi_ref, eta_ref, gamma_ref, charge_ref, resid_ref = refs[:8]
        (fields, geometry, columns, far, blocks, sums, resid, along, *rest) = refs[8:]
        images = rest[:ITERS]
        rest = rest[ITERS:]
        parts = rest[: len(groups)]
        halo_send, halo_recv, sum_send, sum_recv = rest[len(groups) :]

        me = {a: lax.axis_index(a) for a in AXES}

        def neighbour(step):
            return tuple(
                lax.rem(me[a] + (d + sizes[a]), sizes[a]) for a, d in zip(AXES, step)
            )

        def member(axes, hop):
            rank = 0
            count = 1
            for a in axes:
                rank = rank * sizes[a] + me[a]
                count = count * sizes[a]
            rank = lax.rem(rank + hop, count)
            place = dict(me)
            for a in reversed(axes):
                place[a] = lax.rem(rank, sizes[a])
                rank = rank // sizes[a]
            return tuple(place[a] for a in AXES)

        def lookup(kinds, table):
            result = jnp.zeros(kinds.shape, jnp.float32)
            for k in range(types):
                result = jnp.where(kinds == float(k), table[k], result)
            return result

        for x, y, z in local:
            for f in range(3):
                fields[x + 1, y + 1, z + 1, f : f + 1, :] = off_ref[f, x, y, z : z + 1, :]
            fields[x + 1, y + 1, z + 1, 3:4, :] = type_ref[x, y, z : z + 1, :].astype(jnp.float32)

        barrier = pltpu.get_barrier_semaphore()
        greeted = 0
        for axes, count in zip(groups, group_sizes):
            for hop in range(1, count):
                pl.semaphore_signal(
                    barrier, inc=1, device_id=member(axes, hop), device_id_type=MESH
                )
                greeted += 1
        if len(groups) > 1:
            for step in REMOTE:
                pl.semaphore_signal(
                    barrier, inc=1, device_id=neighbour(step), device_id_type=MESH
                )
                greeted += 1
        pl.semaphore_wait(barrier, greeted)

        def halo(buffer, stage):
            copies = []
            for n, step in enumerate(REMOTE):
                source, target = rounded_sides(step, cells)
                copies.append(
                    pltpu.make_async_remote_copy(
                        src_ref=buffer.at[source],
                        dst_ref=buffer.at[target],
                        send_sem=halo_send.at[n],
                        recv_sem=halo_recv.at[stage, n],
                        device_id=neighbour(step),
                        device_id_type=MESH,
                    )
                )
            for copy in copies:
                copy.start()
            return copies

        def finish(copies):
            for copy in copies:
                copy.wait_recv()
            for copy in copies:
                copy.wait_send()

        moving = halo(fields, 0)

        def tenth(values, f, place):
            return (values + CELL_EDGE * (place[f] - 1.0)) * (1.0 / CUTOFF)

        def sigma(kinds):
            root = lax.rsqrt(lookup(kinds, gamma_ref))
            return root * root * root * (CUTOFF**-1.5)

        for t, (x, y, z) in enumerate(local):
            place = (x + 1, y + 1, z + 1)
            for f in range(4):
                row = fields[x + 1, y + 1, z + 1, f : f + 1, :]
                row = tenth(row, f, place) if f < 3 else sigma(row)
                columns[t, f] = jnp.transpose(jnp.broadcast_to(row, (atoms, atoms)))
        entries = jnp.concatenate(
            [list_ref[x, y, z : z + 1, :] - linear((x + 1, y + 1, z + 1)) for x, y, z in local], 0
        )
        for n, step in enumerate(STEPS):
            found = jnp.max(
                jnp.where(entries == linear(step), 1.0, 0.0), axis=1, keepdims=True
            )
            far[n] = jnp.broadcast_to((1.0 - found) * FAR, (tiles, atoms))

        finish(moving)

        for x, y, z in padded:
            place = (x, y, z)
            kinds = fields[x, y, z, 3:4, :]
            for f in range(3):
                geometry[x, y, z, f : f + 1, :] = tenth(fields[x, y, z, f : f + 1, :], f, place)
            geometry[x, y, z, 3:4, :] = sigma(kinds)
            resid[x, y, z, 0:1, :] = -lookup(kinds, chi_ref)
            resid[x, y, z, 1:2, :] = jnp.full((1, atoms), -1.0, jnp.float32)

        slabs = atoms // rows

        def spot(index):
            t = index // slabs
            at = pl.multiple_of((index % slabs) * rows, rows)
            z = t % cells[2]
            y = (t // cells[2]) % cells[1]
            x = t // (cells[2] * cells[1])
            return t, at, (x + 1, y + 1, z + 1)

        def build(index, carry):
            t, at, (x, y, z) = spot(index)
            own_part = [columns[t, f, pl.ds(at, rows), :] for f in range(4)]
            total_s = jnp.zeros((rows, atoms), jnp.float32)
            total_t = jnp.zeros((rows, atoms), jnp.float32)
            for n, (a, b, c) in enumerate(STEPS):
                near = [geometry[x + a, y + b, z + c, f : f + 1, :] for f in range(4)]
                near[0] = near[0] + far[n, pl.ds(t, 1), :]
                dx = near[0] - own_part[0]
                dy = near[1] - own_part[1]
                dz = near[2] - own_part[2]
                square = dx * dx + dy * dy + dz * dz
                if (a, b, c) == (0, 0, 0):
                    i = lax.broadcasted_iota(jnp.int32, (rows, atoms), 0) + at
                    j = lax.broadcasted_iota(jnp.int32, (rows, atoms), 1)
                    square = jnp.where(i == j, 4.0, square)
                u = square * lax.rsqrt(square)
                w = jnp.maximum(1.0 - u, 0.0)
                w = w * w
                w = w * w
                shape = (u + 0.5) * (square + 0.2) - 0.05
                cube = square * u + own_part[3] * near[3]
                block = w * shape * jnp.exp2(jnp.log2(cube) * (-1.0 / 3.0))
                blocks[t, n, pl.ds(at, rows), :] = block
                total_s = total_s + block * resid[x + a, y + b, z + c, 0:1, :]
                total_t = total_t - block
            sums[t, 0, pl.ds(at, rows), :] = total_s
            sums[t, 1, pl.ds(at, rows), :] = total_t
            return carry

        def again(index, carry):
            t, at, (x, y, z) = spot(index)
            total_s = jnp.zeros((rows, atoms), jnp.float32)
            total_t = jnp.zeros((rows, atoms), jnp.float32)
            for n, (a, b, c) in enumerate(STEPS):
                block = blocks[t, n, pl.ds(at, rows), :]
                total_s = total_s + block * resid[x + a, y + b, z + c, 0:1, :]
                total_t = total_t + block * resid[x + a, y + b, z + c, 1:2, :]
            sums[t, 0, pl.ds(at, rows), :] = total_s
            sums[t, 1, pl.ds(at, rows), :] = total_t
            return carry

        scale = 20.0 * COULOMB / CUTOFF
        ones = jnp.ones((8, atoms), jnp.float32)
        eta = [lookup(fields[x + 1, y + 1, z + 1, 3:4, :], eta_ref) for x, y, z in local]

        def collect(image):
            for t, (x, y, z) in enumerate(local):
                for s in range(2):
                    row = lax.dot_general(
                        ones,
                        sums[t, s],
                        (((1,), (1,)), ((), ())),
                        precision=lax.Precision.HIGHEST,
                        preferred_element_type=jnp.float32,
                    )[0:1]
                    here = resid[x + 1, y + 1, z + 1, s : s + 1, :]
                    image[x + 1, y + 1, z + 1, s : s + 1, :] = eta[t] * here + scale * row

        lane = lax.broadcasted_iota(jnp.int32, (2, atoms), 1)

        def over_own(values):
            return jnp.sum(jnp.sum(values, axis=(0, 1, 2)), axis=1, keepdims=True)

        def packed(values):
            message = jnp.zeros((2, atoms), jnp.float32)
            for k, value in enumerate(values):
                message = jnp.where(lane == k, value, message)
            return message

        def start_sum(g, stage):
            axes, count = groups[g], group_sizes[g]
            start = sum(group_sizes[:g]) - g
            copies = []
            for hop in range(1, count):
                copies.append(
                    pltpu.make_async_remote_copy(
                        src_ref=parts[g].at[stage, 0],
                        dst_ref=parts[g].at[stage, hop],
                        send_sem=sum_send.at[start + hop - 1],
                        recv_sem=sum_recv.at[stage, start + hop - 1],
                        device_id=member(axes, hop),
                        device_id_type=MESH,
                    )
                )
            for copy in copies:
                copy.start()
            return copies

        def exchange(values, image, stage):
            parts[0][stage, 0] = packed(values)
            moving = halo(image, stage + 1) if stage + 1 < ITERS else []
            copies = start_sum(0, stage)
            for g in range(len(groups)):
                finish(copies)
                total = jnp.sum(parts[g][stage], axis=0)
                if g + 1 < len(groups):
                    parts[g + 1][stage, 0] = total
                    copies = start_sum(g + 1, stage)
            finish(moving)
            return [
                jnp.sum(jnp.where(lane == k, total, 0.0), axis=1, keepdims=True)
                for k in range(len(values))
            ]

        lax.fori_loop(0, tiles * slabs, build, 0)
        collect(images[0])
        direction = resid[own]
        norm_now, curvature = exchange(
            [over_own(direction * direction), over_own(direction * images[0][own])], images[0], 0
        )
        step_size = norm_now / curvature
        answer = jnp.zeros_like(direction)
        sum_answer = jnp.zeros_like(norm_now)
        along[...] = images[0][...]
        carried = (norm_now, norm_now, norm_now, jnp.zeros_like(norm_now))
        for iteration in range(ITERS):
            answer = answer + step_size * direction
            if iteration + 1 == ITERS:
                last = resid[own] - step_size * along[own]
                break
            resid[...] = resid[...] - step_size * along[...]
            lax.fori_loop(0, tiles * slabs, again, 0)
            image = images[iteration + 1]
            collect(image)
            here = resid[own]
            values = [over_own(here * here), over_own(here * image[own])]
            ends = iteration + 2 == ITERS
            if ends:
                values = values + [over_own(answer), over_own(here), over_own(direction)]
            norm_next, curvature, *others = exchange(values, image, iteration + 1)
            growth = norm_next / norm_now
            step_size = norm_next / (curvature - growth * norm_next / step_size)
            direction = here + growth * direction
            if ends:
                along[own] = image[own] + growth * along[own]
                totals = others[0] + step_size * (others[1] + growth * others[2])
            else:
                along[...] = image[...] + growth * along[...]
            norm_now = norm_next

        level = totals[0:1] / totals[1:2]
        for t, (x, y, z) in enumerate(local):
            charge_ref[x, y, z : z + 1, :] = 1000.0 * (
                answer[x, y, z, 0:1] - level * answer[x, y, z, 1:2]
            )
            for s in range(2):
                resid_ref[s, x, y, z : z + 1, :] = last[x, y, z, s : s + 1]

    scratch = [
        pltpu.VMEM(width + (4, atoms), jnp.float32),
        pltpu.VMEM(width + (4, atoms), jnp.float32),
        pltpu.VMEM((tiles, 4, atoms, atoms), jnp.float32),
        pltpu.VMEM((len(STEPS), tiles, atoms), jnp.float32),
        pltpu.VMEM((tiles, len(STEPS), atoms, atoms), jnp.float32),
        pltpu.VMEM((tiles, 2, atoms, atoms), jnp.float32),
        pltpu.VMEM(width + (2, atoms), jnp.float32),
        pltpu.VMEM(width + (2, atoms), jnp.float32),
    ]
    scratch += [pltpu.VMEM(width + (2, atoms), jnp.float32) for _ in range(ITERS)]
    scratch += [pltpu.VMEM((ITERS, count, 2, atoms), jnp.float32) for count in group_sizes]
    hops = sum(group_sizes) - len(groups)
    scratch += [
        pltpu.SemaphoreType.DMA((len(REMOTE),)),
        pltpu.SemaphoreType.DMA((ITERS, len(REMOTE))),
        pltpu.SemaphoreType.DMA((hops,)),
        pltpu.SemaphoreType.DMA((ITERS, hops)),
    ]
    return kernel, scratch


def solution(mesh):
    sizes = {a: mesh.shape[a] for a in AXES}
    devices = sizes["gx"] * sizes["gy"] * sizes["gz"]
    groups = (AXES,) if devices <= 64 else tuple((a,) for a in AXES)

    def per_device(offsets, type_ids, neighbours, type_chi, type_eta, type_gamma):
        cells = offsets.shape[1:4]
        atoms = offsets.shape[4]
        types = type_chi.shape[0]
        kernel, scratch = make_kernel(sizes, groups, cells, atoms, types, 32)
        vmem = pl.BlockSpec(memory_space=pltpu.VMEM)
        smem = pl.BlockSpec(memory_space=pltpu.SMEM)
        return pl.pallas_call(
            kernel,
            out_shape=(
                jax.ShapeDtypeStruct(cells + (atoms,), jnp.float32),
                jax.ShapeDtypeStruct((2,) + cells + (atoms,), jnp.float32),
            ),
            in_specs=[vmem, vmem, vmem, smem, smem, smem],
            out_specs=(vmem, vmem),
            scratch_shapes=scratch,
            compiler_params=pltpu.CompilerParams(
                collective_id=0, has_side_effects=True, vmem_limit_bytes=48 * 1024 * 1024
            ),
        )(offsets, type_ids, neighbours, type_chi, type_eta, type_gamma)

    placed = (
        P(None, "gx", "gy", "gz", None),
        P("gx", "gy", "gz", None),
        P("gx", "gy", "gz", None),
        P(),
        P(),
        P(),
    )
    return jax.shard_map(
        per_device,
        mesh=mesh,
        in_specs=placed,
        out_specs=(P("gx", "gy", "gz", None), P(None, "gx", "gy", "gz", None)),
        check_vma=False,
    )
```

time: 242 us -> 49.5 us (0.20)
  blocking collectives: 118 us -> 0 us
  Pallas kernels: 0 us -> 43.4 us
  other arithmetic: 33.9 us -> 0 us
  starting transfers between devices: 32.6 us -> 0 us
  matrix products: 25 us -> 0 us
  waiting for transfers between devices: 15.1 us -> 0 us
  local copies, waits for them, and re-layouts: 13.6 us -> 5.18 us
    psum x3 -> x0, blocking collectives: 118 us -> none  [products(): lax.psum((summed_over(residual * residual), summed_over(residual * image_...]
    pallas_call x0 -> x1, Pallas kernels: none -> 43.4 us  [per_device(): pl.pallas_call(kernel, out_shape=(jax.ShapeDtypeStruct(cells + (atoms,),...]
    ppermute x24 -> x0, starting transfers between devices: 32.6 us -> none  [the longest x12 16.5 us: extended(): lax.ppermute(tail, axis, [(i, (i + 1) % count) for i in range(count)])]
    dot_general x3 -> x0, matrix products: 25 us -> none  [apply_padded(): jnp.einsum('tsij,ctsj->cti', blocks, values, precision=lax.Precision.HIGH...]
    dynamic_update_slice x4 -> x0, other arithmetic: 17.9 us -> none  [per_device(): lax.map(build_tile, (own_pos, own_shield, row_index, shifts, listed, itse...]
    ppermute x24 -> x0, waiting for transfers between devices: 15.1 us -> none  [the longest x12 9.78 us: extended(): lax.ppermute(tail, axis, [(i, (i + 1) % count) for i in range(count)])]
    select_n x6 -> x0, other arithmetic: 7.86 us -> none  [the longest x1 4.42 us: table_lookup(): result = jnp.where(type_ids == kind_index, table[kind_index], result)]
    gather x11 -> x0, local copies, waits for them, and re-layouts: 6.83 us -> none  [the longest x4 2.41 us: build_tile(): pos_all[:, indices]]
  transfers between devices with their start and end apart: 24 -> 0, of which waited for: 12 -> 0; matrix products, arithmetic and copies ran while one was open for 2% -> 0% of each run, Pallas kernels for 0% -> 0%
where the time goes in v1:
time: 49.5 us; the launch traced here: 49.2 us
  Pallas kernels  43.4 us (88%)
  local copies, waits for them, and re-layouts  5.18 us (10%)
  between operations  0.65 us (1%)
    pallas_call x1, Pallas kernels, per_device(): pl.pallas_call(kernel, out_shape=(jax.ShapeDtypeStruct(cells + (atoms,),...  43.4 us
    unnamed x14, local copies, waits for them, and re-layouts  5.18 us

profile of v1, /device:TPU:0, one launch (start us, length us, event | category | flops | bytes accessed | tf_op | source)
XLA Modules:
  0.0 49.2 jit_solution(9065795859513179252)
XLA Ops:
  0.6 0.0 copy-start
  0.6 0.7 %copy-done = f32[3,1,2,2,128]{4,3,2,1,0:T(2,128)S(1)} copy-done((f32[3,1,2,2,128]{4,3,2,1,0:T(2,128)S(1)}, f32[3,1,2,2,128]{4,3,2,1,0:T(2,128)}, u32[]{:S(2)}) %copy-start) | copy-done | bytes 6168
  1.3 0.0 copy-start.1
  1.3 0.7 %copy-done.1 = s32[1,2,2,128]{3,2,1,0:T(2,128)S(1)} copy-done((s32[1,2,2,128]{3,2,1,0:T(2,128)S(1)}, s32[1,2,2,128]{3,2,1,0:T(2,128)}, u32[]{:S(2)}) %copy-start.1) | copy-done | bytes 2072
  2.0 0.0 copy-start.2
  2.0 0.7 %copy-done.2 = s32[1,2,2,27]{3,2,1,0:T(2,128)S(1)} copy-done((s32[1,2,2,27]{3,2,1,0:T(2,128)S(1)}, s32[1,2,2,27]{3,2,1,0:T(2,128)}, u32[]{:S(2)}) %copy-start.2) | copy-done | bytes 456
  2.7 0.0 copy-start.3
  2.7 0.7 %copy-done.3 = f32[2]{0:T(128)S(1)} copy-done((f32[2]{0:T(128)S(1)}, f32[2]{0:T(128)}, u32[]{:S(2)}) %copy-start.3) | copy-done | bytes 32
  3.3 0.0 copy-start.4
  3.3 0.7 %copy-done.4 = f32[2]{0:T(128)S(1)} copy-done((f32[2]{0:T(128)S(1)}, f32[2]{0:T(128)}, u32[]{:S(2)}) %copy-start.4) | copy-done | bytes 32
  4.0 0.0 copy-start.5
  4.0 0.7 %copy-done.5 = f32[2]{0:T(128)S(1)} copy-done((f32[2]{0:T(128)S(1)}, f32[2]{0:T(128)}, u32[]{:S(2)}) %copy-start.5) | copy-done | bytes 32
  4.7 43.4 %shard_map.77 = (f32[1,2,2,128]{3,2,1,0:T(2,128)S(1)}, f32[2,1,2,2,128]{4,3,2,1,0:T(2,128)S(1)}) custom-call(f32[3,1,2,2,128]{4,3,2,1,0:T(2,128)S(1)} %copy-done, s32[1,2,2,128]{3,2,1,0:T(2,128)S(1)} %copy-done.1, s32[1,2,2,27]{3,2,1,0:T(2,128)S(1)} %copy-done.2, f32[2]{0:T(128)S(1)} %copy-done.3, f32[2]{0:T(128)S(1)} %copy-done.4, f32[2]{0:T(128)S(1)} %copy-done.5), custom_call_target="tpu_custom_call" | custom-call | tf_op jit(solution)/shard_map/pallas_call | solution.py:359
  48.0 0.6 %copy.10 = f32[1,2,2,128]{3,2,1,0:T(2,128)} copy(f32[1,2,2,128]{3,2,1,0:T(2,128)S(1)} %get-tuple-element.4) | data formatting | bytes 4096
  48.6 0.6 %copy.11 = f32[2,1,2,2,128]{4,3,2,1,0:T(2,128)} copy(f32[2,1,2,2,128]{4,3,2,1,0:T(2,128)S(1)} %get-tuple-element.5) | data formatting | bytes 8192
Async XLA Ops:
  0.6 0.7 %copy-start = (f32[3,1,2,2,128]{4,3,2,1,0:T(2,128)S(1)}, f32[3,1,2,2,128]{4,3,2,1,0:T(2,128)}, u32[]{:S(2)}) copy-start(f32[3,1,2,2,128]{4,3,2,1,0:T(2,128)} %refs_0_.1) | copy-start | bytes 18436
  1.3 0.7 %copy-start.1 = (s32[1,2,2,128]{3,2,1,0:T(2,128)S(1)}, s32[1,2,2,128]{3,2,1,0:T(2,128)}, u32[]{:S(2)}) copy-start(s32[1,2,2,128]{3,2,1,0:T(2,128)} %refs_1_.1) | copy-start | bytes 6148
  2.0 0.7 %copy-start.2 = (s32[1,2,2,27]{3,2,1,0:T(2,128)S(1)}, s32[1,2,2,27]{3,2,1,0:T(2,128)}, u32[]{:S(2)}) copy-start(s32[1,2,2,27]{3,2,1,0:T(2,128)} %refs_2_.1) | copy-start | bytes 1300
  2.7 0.7 %copy-start.3 = (f32[2]{0:T(128)S(1)}, f32[2]{0:T(128)}, u32[]{:S(2)}) copy-start(f32[2]{0:T(128)} %refs_3_.1) | copy-start | bytes 28
  3.3 0.7 %copy-start.4 = (f32[2]{0:T(128)S(1)}, f32[2]{0:T(128)}, u32[]{:S(2)}) copy-start(f32[2]{0:T(128)} %refs_4_.1) | copy-start | bytes 28
  4.0 0.7 %copy-start.5 = (f32[2]{0:T(128)S(1)}, f32[2]{0:T(128)}, u32[]{:S(2)}) copy-start(f32[2]{0:T(128)} %refs_5_.1) | copy-start | bytes 28
